TPU v7x, 32 devices: a whole 2x2x4 slice. The times are simulated.
32 devices in a mesh: ctx: 16 (over z, y, x), tp: 2 (over core).
Axes of the slice: x: 2, y: 2, z: 4, core: 2. Of those that a mesh axis runs over, the one named last changes fastest.
Arguments:
- queries: bfloat16 [1024, 2560], P('ctx', 'tp'), may hold values from -100 to 100
- projected_keys: bfloat16 [1024, 512], P('ctx', 'tp'), may hold values from -30 to 30
- projected_values: bfloat16 [1024, 512], P('ctx', 'tp'), may hold values from -6 to 6
- hidden: bfloat16 [1024, 5120], P('ctx', 'tp'), may hold values from -6 to 6
- route_ids: int32 [1024, 1], P('ctx'), may hold values from 0 to 15; in each aligned block of 64 rows (0 to 63, 64 to 127, ...) at most 6 rows name the same one
- route_gain: float32 [1024], P('ctx'), may hold values from 0.25 to 1
- w_gate: bfloat16 [16, 5120, 4096], P('ctx', None, 'tp'), may hold values from -0.078125 to 0.078125
- w_up: bfloat16 [16, 5120, 4096], P('ctx', None, 'tp'), may hold values from -0.078125 to 0.078125
- w_down: bfloat16 [16, 4096, 5120], P('ctx', None, 'tp'), may hold values from -0.09375 to 0.09375
Outputs:
- attended: bfloat16 [1024, 2560], P('ctx', 'tp')
- mixed: bfloat16 [1024, 5120], P('ctx', 'tp')
Inputs may be any that keep to these rules, and one draw needn't show every extreme that they name: `route_ids`: within the rows of one device (aligned blocks of 64 rows) no expert is named more than 6 times, a bound that some block reaches.
All inputs are finite; a program needn't handle non-finite values.
Results may differ from a plain program's by a relative error of at most 0.0057.
Values may be sent and summed in bfloat16 or wider, within the bound.
No kernel may reach another device: no remote copies, remote signals or barrier semaphores. Data moves between devices by JAX's collectives and lax.ppermute only.
A program may use at most 128 MiB of HBM per device.

v0:
```python
import math
import jax
import jax.numpy as jnp
from jax import lax
from jax.sharding import PartitionSpec as P

HEAD_SIZE = 128
EXPERTS = 16
CAP = 6
masked_score = -1e30


def body(
    queries, projected_keys, projected_values, hidden, route_ids, route_gain, w_gate, w_up, w_down
):
    tok_rows = queries.shape[0]
    width_q = queries.shape[1]
    width_kv = projected_keys.shape[1]
    ctx_count = lax.axis_size("ctx")
    ctx_index = lax.axis_index("ctx")
    offsets = jnp.arange(tok_rows, dtype=jnp.int32)
    query_use, key_use, value_use = (queries, projected_keys, projected_values)

    def position(device, offset):
        return device * tok_rows + offset

    query_pos = position(ctx_index, offsets)
    query_top = jnp.max(query_pos)
    kv_heads = width_kv // HEAD_SIZE
    head_group = width_q // HEAD_SIZE // kv_heads
    query_tensor = query_use.reshape(tok_rows, kv_heads, head_group, HEAD_SIZE)
    score_scale = HEAD_SIZE ** (-0.5)
    key_whole, value_whole = (
        lax.all_gather(key_use, "ctx", axis=0, tiled=True),
        lax.all_gather(value_use, "ctx", axis=0, tiled=True),
    )
    total_rows = key_whole.shape[0]
    block_rows = math.gcd(total_rows, 1024)

    def absorb_block(block_index, state):
        block_start = block_index * block_rows
        key_block = lax.dynamic_slice_in_dim(key_whole, block_start, block_rows, 0).reshape(
            block_rows, kv_heads, HEAD_SIZE
        )
        value_block = lax.dynamic_slice_in_dim(value_whole, block_start, block_rows, 0).reshape(
            block_rows, kv_heads, HEAD_SIZE
        )
        global_rows = block_start + jnp.arange(block_rows, dtype=jnp.int32)
        key_pos = position(global_rows // tok_rows, global_rows % tok_rows)

        def update(inner_state):
            running_max, running_sum, running_out = inner_state
            scores = (
                jnp.einsum(
                    "qhgd,khd->hgqk", query_tensor, key_block, preferred_element_type=jnp.float32
                )
                * score_scale
            )
            allowed = query_pos[:, None] >= key_pos[None, :]
            scores = jnp.where(allowed, scores, masked_score)
            new_max = jnp.maximum(running_max, jnp.max(scores, axis=3))
            weights = jnp.where(allowed, jnp.exp(scores - new_max[..., None]), 0.0)
            factor = jnp.exp(running_max - new_max)
            new_sum = running_sum * factor + jnp.sum(weights, axis=3)
            partial_out = jnp.einsum(
                "hgqk,khd->qhgd",
                weights.astype(jnp.bfloat16),
                value_block,
                preferred_element_type=jnp.float32,
            )
            new_out = running_out * jnp.transpose(factor, (2, 0, 1))[..., None] + partial_out
            return (new_max, new_sum, new_out)

        def keep_state(inner_state):
            return inner_state

        return lax.cond(jnp.min(key_pos) <= query_top, update, keep_state, state)

    initial = (
        jnp.full((kv_heads, head_group, tok_rows), masked_score, jnp.float32),
        jnp.zeros((kv_heads, head_group, tok_rows), jnp.float32),
        jnp.zeros((tok_rows, kv_heads, head_group, HEAD_SIZE), jnp.float32),
    )
    running_max, running_sum, running_out = lax.fori_loop(
        0, total_rows // block_rows, absorb_block, initial
    )
    attended = (
        (running_out / jnp.transpose(running_sum, (2, 0, 1))[..., None])
        .reshape(tok_rows, width_q)
        .astype(jnp.bfloat16)
    )
    ids_flat = route_ids[:, 0]
    chosen = (ids_flat[:, None] == jnp.arange(EXPERTS, dtype=jnp.int32)[None, :]).astype(jnp.int32)
    ranking = jnp.sum((jnp.cumsum(chosen, axis=0) - chosen) * chosen, axis=1)
    slot_of = ids_flat * CAP + ranking
    selector = (jnp.arange(EXPERTS * CAP, dtype=jnp.int32)[:, None] == slot_of[None, :]).astype(
        jnp.bfloat16
    )
    host_count = ctx_count // EXPERTS
    feature_width = hidden.shape[1]
    packed = jnp.dot(selector, hidden, preferred_element_type=jnp.float32).astype(jnp.bfloat16)
    packed = jnp.broadcast_to(
        packed.reshape(EXPERTS, 1, CAP, feature_width), (EXPERTS, host_count, CAP, feature_width)
    ).reshape(ctx_count, CAP, feature_width)
    arrived = lax.all_to_all(packed, "ctx", split_axis=0, concat_axis=0, tiled=True)
    arrived = lax.all_gather(arrived, "tp", axis=2, tiled=True)
    slot_count = arrived.shape[1]
    flat_rows = arrived.reshape(-1, arrived.shape[2])
    gate_val = jnp.dot(flat_rows, w_gate[0], preferred_element_type=jnp.float32)
    up_val = jnp.dot(flat_rows, w_up[0], preferred_element_type=jnp.float32)
    inner = (jax.nn.silu(gate_val) * up_val).astype(jnp.bfloat16)
    pair_inner = lax.all_gather(inner, "tp", axis=1, tiled=True)
    partial_out = jnp.dot(pair_inner, w_down[0], preferred_element_type=jnp.float32).astype(
        jnp.bfloat16
    )
    partial_out = partial_out.reshape(ctx_count, slot_count, partial_out.shape[1])
    returned = lax.all_to_all(partial_out, "ctx", split_axis=0, concat_axis=0, tiled=True)
    out_width = returned.shape[2]
    summed = returned.reshape(EXPERTS, host_count, CAP, out_width).astype(jnp.float32).sum(axis=1)
    summed = summed.reshape(EXPERTS * CAP, out_width)
    mixed = (summed[slot_of] * route_gain[:, None]).astype(jnp.bfloat16)
    return (attended, mixed)


def solution(mesh):
    in_specs = (
        P("ctx", "tp"),
        P("ctx", "tp"),
        P("ctx", "tp"),
        P("ctx", "tp"),
        P("ctx", None),
        P("ctx"),
        P("ctx", None, "tp"),
        P("ctx", None, "tp"),
        P("ctx", None, "tp"),
    )
    out_specs = (P("ctx", "tp"), P("ctx", "tp"))
    return jax.shard_map(body, mesh=mesh, in_specs=in_specs, out_specs=out_specs, check_vma=False)
```

profile of v0, /device:TPU:0, one launch (start us, length us, event | category | flops | bytes accessed | tf_op | source)
XLA Modules:
  0.0 152.1 jit_solution(1355597205857069275)
XLA Ops:
  0.7 0.8 fusion.35
  1.5 0.8 select_reduce_fusion
  2.4 0.7 multiply_add_fusion.1
  3.3 1.0 reshape_reshape.3
  4.3 8.3 %all-to-all-start = ((bf16[16,6,2560]{2,1,0:T(8,128)(2,1)}), bf16[16,6,2560]{2,1,0:T(8,128)(2,1)S(1)}, u32[]{:S(2)}, u32[]{:S(2)}) async-start(bf16[16,6,2560]{2,1,0:T(8,128)(2,1)} %reshape_reshape.3), calls=%async_computation | async-start | bytes 1310720 | tf_op jit(solution)/shard_map/all_to_all | solution.py:105
  12.7 0.6 fusion.48
  13.3 0.6 fusion.46
  15.3 45.2 %all_gather.12 = bf16[1024,256]{1,0:T(8,128)(2,1)S(1)} all-gather(bf16[64,256]{1,0:T(8,128)(2,1)S(1)} %copy-done.4), channel_id=1, replica_groups=mesh['ctx'=16,'tp'=2] {'ctx'}, dimensions={0}, use_global_device_ids=true | all-gather | bytes 557056 | tf_op jit(solution)/shard_map/all_gather | solution.py:34
  60.5 2.7 %all_gather.14 = bf16[16,6,5120]{2,1,0:T(8,128)(2,1)S(1)} all-gather(bf16[16,6,2560]{2,1,0:T(8,128)(2,1)S(1)} %all-to-all-done), channel_id=1, replica_groups=mesh['ctx'=16,'tp'=2] {'tp'}, dimensions={2}, use_global_device_ids=true | all-gather | bytes 1474560 | tf_op jit(solution)/shard_map/all_gather | solution.py:106
  63.7 8.9 %fusion.24 = f32[96,2048]{1,0:T(8,128)S(1)} fusion(bf16[96,5120]{1,0:T(8,128)(2,1)S(1)} %reshape.55, bf16[1,5120,2048]{2,1,0:T(8,128)(2,1)} %param.17), kind=kOutput, calls=%fused_computation.26 | convolution fusion | flops 2013265920 | bytes 22740992 | tf_op jit(solution)/shard_map/dot_general | solution.py:109
  72.6 11.1 %fusion.32 = bf16[96,2048]{1,0:T(8,128)(2,1)S(1)} fusion(bf16[96,5120]{1,0:T(8,128)(2,1)S(1)} %reshape.55, bf16[1,5120,2048]{2,1,0:T(8,128)(2,1)} %param.18, f32[96,2048]{1,0:T(8,128)S(1)} %fusion.24), kind=kOutput, calls=%fused_computation.31 | convolution fusion | flops 2014445568 | bytes 23134208 | tf_op jit(solution)/shard_map/dot_general | solution.py:110
  83.7 2.4 %all_gather.15 = bf16[96,4096]{1,0:T(8,128)(2,1)S(1)} all-gather(bf16[96,2048]{1,0:T(8,128)(2,1)S(1)} %fusion.32), channel_id=1, replica_groups=mesh['ctx'=16,'tp'=2] {'tp'}, dimensions={1}, use_global_device_ids=true | all-gather | bytes 1179648 | tf_op jit(solution)/shard_map/all_gather | solution.py:112
  86.2 3.4 %fusion.26 = bf16[96,2560]{1,0:T(8,128)(2,1)S(1)} fusion(bf16[96,4096]{1,0:T(8,128)(2,1)S(1)} %all_gather.15, bf16[1,4096,2560]{2,1,0:T(8,128)(2,1)S(1)} %bitcast.52), kind=kOutput, calls=%fused_computation.28 | convolution fusion | flops 2013511680 | bytes 22249472 | tf_op jit(solution)/shard_map/dot_general | solution.py:113
  89.6 1.0 reshape.56
  90.6 3.6 %all-to-all-start.1 = ((bf16[16,6,2560]{2,1,0:T(8,128)(2,1)}), bf16[16,6,2560]{2,1,0:T(8,128)(2,1)S(1)}, u32[]{:S(2)}, u32[]{:S(2)}) async-start(bf16[16,6,2560]{2,1,0:T(8,128)(2,1)} %reshape.56), calls=%async_computation.1 | async-start | bytes 1310720 | tf_op jit(solution)/shard_map/all_to_all | solution.py:117
  94.2 48.7 %all_gather.13 = bf16[1024,256]{1,0:T(8,128)(2,1)S(1)} all-gather(bf16[64,256]{1,0:T(8,128)(2,1)S(1)} %copy-done.5), channel_id=1, replica_groups=mesh['ctx'=16,'tp'=2] {'ctx'}, dimensions={0}, use_global_device_ids=true | all-gather | bytes 557056 | tf_op jit(solution)/shard_map/all_gather | solution.py:35
  142.9 6.3 %conditional.1 = ((f32[2,5,64]{2,1,0:T(8,128)S(1)}, f32[64,2,5,128]{3,0,2,1:T(8,128)S(1)})) conditional(s32[]{:T(128)} %convert_element_type.33, (f32[2,5,64]{2,1,0:T(8,128)S(1)}, f32[64,2,5,128]{3,0,2,1:T(8,128)S(1)}) %tuple.25, (s32[64]{0:T(128)S(1)}, s32[1024]{0:T(1024)S(1)}, bf16[1024,256]{1,0:T(8,128)(2,1)S(1)}, bf16[64,1280]{1,0:T(8,128)(2,1)S(1)}, ...), branch_computations={%region_2.3_spmd, %region_3.6_spmd} | conditional | flops 344295296 | bytes 22939956 | solution.py:77
  143.3 0.7 fusion
  144.0 1.5 copy-done.2
  145.5 0.8 fusion.2
  146.5 2.6 %fusion.9 = f32[64,2,5,128]{3,0,2,1:T(8,128)S(1)} fusion(f32[2,1024,64,5]{1,2,3,0:T(8,128)} %copy-done.2, f32[2,5,64]{2,1,0:T(8,128)S(1)} %broadcast_maximum_fusion, pred[64,1024]{1,0:T(8,128)(4,1)S(1)} %broadcast_compare_fusion, bf16[1024,2,128,1]{2,1,0,3:T(2,128)(2,1)S(1)} %bitcast.53, f32[64,2,5,128]{3,0,2,1:T(8,128)S(1)} %get-tuple-element.89, ...), kind=kOutput, calls=%fused_computation.9 | convolution fusion | flops 171212800 | bytes 3871744 | tf_op jit(solution)/shard_map/while/body/eval_jaxpr/cond/branch_1_fun/hgqk,khd->qhgd/dot_general | solution.py:65
  149.4 0.9 convert_element_type.35
  150.5 0.8 gather_fusion
  151.3 0.8 multiply_convert_fusion
  (46 shorter events, 1.8 us)
Async XLA Ops:
  0.6 2.4 %copy-start = (bf16[64,2560]{1,0:T(8,128)(2,1)S(1)}, bf16[64,2560]{1,0:T(8,128)(2,1)}, u32[]{:S(2)}) copy-start(bf16[64,2560]{1,0:T(8,128)(2,1)} %param.14) | copy-start | bytes 983044
  0.6 14.6 %copy-start.4 = (bf16[64,256]{1,0:T(8,128)(2,1)S(1)}, bf16[64,256]{1,0:T(8,128)(2,1)}, u32[]{:S(2)}) copy-start(bf16[64,256]{1,0:T(8,128)(2,1)} %param.12) | copy-start | bytes 98308
  4.3 56.2 %all-to-all-start = ((bf16[16,6,2560]{2,1,0:T(8,128)(2,1)}), bf16[16,6,2560]{2,1,0:T(8,128)(2,1)S(1)}, u32[]{:S(2)}, u32[]{:S(2)}) async-start(bf16[16,6,2560]{2,1,0:T(8,128)(2,1)} %reshape_reshape.3), calls=%async_computation | async-start | bytes 1310720 | tf_op jit(solution)/shard_map/all_to_all | solution.py:105
  63.6 22.5 %slice-start = ((s8[20971520]{0:T(1024)(128)(4,1)}), s8[4194304]{0:T(1024)(128)(4,1)S(1)}, s32[]{:S(2)}) async-start(s8[20971520]{0:T(1024)(128)(4,1)} %bitcast.51), calls=%async_computation.2 | async-start | bytes 8388608
  63.6 22.5 %slice-start.1 = ((s8[20971520]{0:T(1024)(128)(4,1)}), s8[4194304]{0:T(1024)(128)(4,1)S(1)}, s32[]{:S(2)}) async-start(s8[20971520]{0:T(1024)(128)(4,1)} %bitcast.51), calls=%async_computation.3 | async-start | bytes 8388608
  63.7 22.5 %slice-start.2 = ((s8[20971520]{0:T(1024)(128)(4,1)}), s8[4194304]{0:T(1024)(128)(4,1)S(1)}, s32[]{:S(2)}) async-start(s8[20971520]{0:T(1024)(128)(4,1)} %bitcast.51), calls=%async_computation.4 | async-start | bytes 8388608
  72.6 13.5 %slice-start.3 = ((s8[20971520]{0:T(1024)(128)(4,1)}), s8[4194304]{0:T(1024)(128)(4,1)S(1)}, s32[]{:S(2)}) async-start(s8[20971520]{0:T(1024)(128)(4,1)} %bitcast.51), calls=%async_computation.5 | async-start | bytes 8388608
  72.6 13.5 %slice-start.4 = ((s8[20971520]{0:T(1024)(128)(4,1)}), s8[4194304]{0:T(1024)(128)(4,1)S(1)}, s32[]{:S(2)}) async-start(s8[20971520]{0:T(1024)(128)(4,1)} %bitcast.51), calls=%async_computation.6 | async-start | bytes 8388608
  86.2 8.1 %copy-start.5 = (bf16[64,256]{1,0:T(8,128)(2,1)S(1)}, bf16[64,256]{1,0:T(8,128)(2,1)}, u32[]{:S(2)}) copy-start(bf16[64,256]{1,0:T(8,128)(2,1)} %param.13) | copy-start | bytes 98308
  89.6 53.3 %copy-start.3 = (bf16[64,1280]{1,0:T(8,128)(2,1)S(1)}, bf16[64,1280]{1,0:T(8,128)(2,1)}, u32[]{:S(2)}) copy-start(bf16[64,1280]{1,0:T(8,128)(2,1)} %param.11) | copy-start | bytes 491524
  90.6 59.7 %all-to-all-start.1 = ((bf16[16,6,2560]{2,1,0:T(8,128)(2,1)}), bf16[16,6,2560]{2,1,0:T(8,128)(2,1)S(1)}, u32[]{:S(2)}, u32[]{:S(2)}) async-start(bf16[16,6,2560]{2,1,0:T(8,128)(2,1)} %reshape.56), calls=%async_computation.1 | async-start | bytes 1310720 | tf_op jit(solution)/shard_map/all_to_all | solution.py:117
  142.9 7.4 %copy-start.6 = (s32[64,1]{0,1:T(1,128)S(1)}, s32[64,1]{0,1:T(1,128)}, u32[]{:S(2)}) copy-start(s32[64,1]{0,1:T(1,128)} %param.15) | copy-start | bytes 772
  144.0 1.5 copy-start.2
  150.3 1.8 %copy-start.1 = (bf16[64,2560]{1,0:T(8,128)(2,1)S(1)}, bf16[64,2560]{1,0:T(8,128)(2,1)}, u32[]{:S(2)}) copy-start(bf16[64,2560]{1,0:T(8,128)(2,1)} %param.14) | copy-start | bytes 983044
  150.5 0.8 copy-start.7
where the time goes:
time: 153 us; the launch traced here: 152 us
  blocking collectives  99 us (65%)
  matrix products  27 us (18%)
  starting transfers between devices  11.9 us (8%)
  local copies, waits for them, and re-layouts  6.33 us (4%)
  other arithmetic  5.61 us (4%)
  between operations  2.2 us (1%)
    all_gather x1, blocking collectives, body(): lax.all_gather(value_use, 'ctx', axis=0, tiled=True)  48.7 us
    all_gather x1, blocking collectives, body(): lax.all_gather(key_use, 'ctx', axis=0, tiled=True)  45.2 us
    dot_general x1, matrix products, body(): up_val = jnp.dot(flat_rows, w_up[0], preferred_element_type=jnp.float32)  11.1 us
    dot_general x1, matrix products, body(): gate_val = jnp.dot(flat_rows, w_gate[0], preferred_element_type=jnp.float32)  8.92 us
    all_to_all x1, starting transfers between devices, body(): lax.all_to_all(packed, 'ctx', split_axis=0, concat_axis=0, tiled=True)  8.34 us
    all_to_all x1, starting transfers between devices, body(): lax.all_to_all(partial_out, 'ctx', split_axis=0, concat_axis=0, tiled=True)  3.59 us
    dot_general x1, matrix products, body(): jnp.dot(pair_inner, w_down[0], preferred_element_type=jnp.float32)  3.41 us
  transfers between devices with their start and end apart: 2, of which 0 were waited for; matrix products, arithmetic and copies ran while one was open for 5% of the time, Pallas kernels for 0%

commit v1 on v0

--- a/solution.py
+++ b/solution.py
@@ -8,6 +8,18 @@
 EXPERTS = 16
 CAP = 6
 masked_score = -1e30
+
+
+def doubled_up(shard, axis, dim):
+    ways, here, step = (lax.axis_size(axis), lax.axis_index(axis), shard.shape[dim])
+    line, have = (shard, 1)
+    while have < ways:
+        line = jnp.concatenate(
+            [line, lax.ppermute(line, axis, [(d, (d - have) % ways) for d in range(ways)])],
+            axis=dim,
+        )
+        have = 2 * have
+    return jnp.roll(line, here * step, axis=dim)
 
 
 def body(
@@ -32,7 +44,7 @@
     score_scale = HEAD_SIZE ** (-0.5)
     key_whole, value_whole = (
         lax.all_gather(key_use, "ctx", axis=0, tiled=True),
-        lax.all_gather(value_use, "ctx", axis=0, tiled=True),
+        doubled_up(value_use, "ctx", 0),
     )
     total_rows = key_whole.shape[0]
     block_rows = math.gcd(total_rows, 1024)

time: 153 us -> 139 us (0.908)
  blocking collectives: 99 us -> 53.8 us
  starting transfers between devices: 11.9 us -> 30 us
  waiting for transfers between devices: 0.01 us -> 11.3 us
  local copies, waits for them, and re-layouts: 6.33 us -> 8.18 us
    all_gather x1 -> x0, blocking collectives: 48.7 us -> none  [body(): lax.all_gather(value_use, 'ctx', axis=0, tiled=True)]
    ppermute x0 -> x4, starting transfers between devices: none -> 12.1 us  [doubled_up(): lax.ppermute(line, axis, [(d, (d - have) % ways) for d in range(ways)])]
    ppermute x0 -> x4, waiting for transfers between devices: none -> 11.3 us  [doubled_up(): lax.ppermute(line, axis, [(d, (d - have) % ways) for d in range(ways)])]
    all_to_all x1, starting transfers between devices: 3.59 us -> 9.59 us  [body(): lax.all_to_all(partial_out, 'ctx', split_axis=0, concat_axis=0, tiled=True)]
    all_gather x1, blocking collectives: 45.2 us -> 48.7 us  [body(): lax.all_gather(key_use, 'ctx', axis=0, tiled=True)]
    concatenate x0 -> x1, local copies, waits for them, and re-layouts: none -> 1.63 us  [doubled_up(): return jnp.roll(line, here * step, axis=dim)]
  transfers between devices with their start and end apart: 2 -> 6, of which waited for: 0 -> 2; matrix products, arithmetic and copies ran while one was open for 5% -> 25% of each run, Pallas kernels for 0% -> 0%
where the time goes in v1:
time: 139 us
  blocking collectives  53.8 us (39%)
  starting transfers between devices  30 us (22%)
  matrix products  27 us (19%)
  waiting for transfers between devices  11.3 us (8%)
  local copies, waits for them, and re-layouts  8.18 us (6%)
  other arithmetic  5.93 us (4%)
  between operations  2.16 us (2%)
    all_gather x1, blocking collectives, body(): lax.all_gather(key_use, 'ctx', axis=0, tiled=True)  48.7 us
    ppermute x4, starting transfers between devices, doubled_up(): lax.ppermute(line, axis, [(d, (d - have) % ways) for d in range(ways)])  12.1 us
    ppermute x4, waiting for transfers between devices, doubled_up(): lax.ppermute(line, axis, [(d, (d - have) % ways) for d in range(ways)])  11.3 us
    dot_general x1, matrix products, body(): up_val = jnp.dot(flat_rows, w_up[0], preferred_element_type=jnp.float32)  11.1 us
    all_to_all x1, starting transfers between devices, body(): lax.all_to_all(partial_out, 'ctx', split_axis=0, concat_axis=0, tiled=True)  9.59 us
    dot_general x1, matrix products, body(): gate_val = jnp.dot(flat_rows, w_gate[0], preferred_element_type=jnp.float32)  8.92 us
    all_to_all x1, starting transfers between devices, body(): lax.all_to_all(packed, 'ctx', split_axis=0, concat_axis=0, tiled=True)  8.34 us
    dot_general x1, matrix products, body(): jnp.dot(pair_inner, w_down[0], preferred_element_type=jnp.float32)  3.41 us
  transfers between devices with their start and end apart: 6, of which 2 were waited for; matrix products, arithmetic and copies ran while one was open for 25% of the time, Pallas kernels for 0%

profile of v1, /device:TPU:0, one launch (start us, length us, event | category | flops | bytes accessed | tf_op | source)
XLA Modules:
  0.0 138.7 jit_solution(10570017225256986352)
XLA Ops:
  1.5 0.8 select_reduce_fusion
  3.3 1.0 reshape_reshape.3
  4.3 8.3 %all-to-all-start = ((bf16[16,6,2560]{2,1,0:T(8,128)(2,1)}), bf16[16,6,2560]{2,1,0:T(8,128)(2,1)S(1)}, u32[]{:S(2)}, u32[]{:S(2)}) async-start(bf16[16,6,2560]{2,1,0:T(8,128)(2,1)} %reshape_reshape.3), calls=%async_computation | async-start | bytes 1310720 | tf_op jit(solution)/shard_map/all_to_all | solution.py:117
  12.8 5.6 %collective-permute-start = (bf16[64,256]{0,1:T(8,128)(2,1)S(1)}, bf16[64,256]{0,1:T(8,128)(2,1)S(1)}, u32[]{:S(2)}, u32[]{:S(2)}) collective-permute-start(bf16[64,256]{0,1:T(8,128)(2,1)S(1)} %copy.23), channel_id=1, source_target_pairs={{0,30},{2,0},{4,2},{6,4},{8,6},{10,8},{12,10},{14,12},{16,14},{18,... | collective-permute-start | bytes 98312 | tf_op jit(solution)/shard_map/ppermute | solution.py:18
  18.4 6.8 %collective-permute-done = bf16[64,256]{0,1:T(8,128)(2,1)S(1)} collective-permute-done((bf16[64,256]{0,1:T(8,128)(2,1)S(1)}, bf16[64,256]{0,1:T(8,128)(2,1)S(1)}, u32[]{:S(2)}, u32[]{:S(2)}) %collective-permute-start) | collective-permute-done | bytes 32800 | tf_op jit(solution)/shard_map/ppermute | solution.py:18
  25.3 4.6 %collective-permute-done.1 = bf16[128,256]{0,1:T(8,128)(2,1)S(1)} collective-permute-done((bf16[128,256]{0,1:T(8,128)(2,1)S(1)}, bf16[128,256]{0,1:T(8,128)(2,1)S(1)}, u32[]{:S(2)}, u32[]{:S(2)}) %collective-permute-start.1) | collective-permute-done | bytes 65568 | tf_op jit(solution)/shard_map/ppermute | solution.py:18
  30.0 3.5 %collective-permute-start.2 = (bf16[256,256]{0,1:T(8,128)(2,1)S(1)}, bf16[256,256]{0,1:T(8,128)(2,1)S(1)}, u32[]{:S(2)}, u32[]{:S(2)}) collective-permute-start(bf16[256,256]{0,1:T(8,128)(2,1)S(1)} %pad_maximum_fusion.1), channel_id=1, source_target_pairs={{0,24},{2,26},{4,28},{6,30},{8,0},{10,2},{12,4},{14,6},{16,8},{18,... | collective-permute-start | bytes 393224 | tf_op jit(solution)/shard_map/ppermute | solution.py:18
  33.6 2.7 %all_gather.10 = bf16[16,6,5120]{2,1,0:T(8,128)(2,1)S(1)} all-gather(bf16[16,6,2560]{2,1,0:T(8,128)(2,1)S(1)} %all-to-all-done), channel_id=1, replica_groups=mesh['ctx'=16,'tp'=2] {'tp'}, dimensions={2}, use_global_device_ids=true | all-gather | bytes 1474560 | tf_op jit(solution)/shard_map/all_gather | solution.py:118
  36.7 8.9 %fusion.23 = f32[96,2048]{1,0:T(8,128)S(1)} fusion(bf16[96,5120]{1,0:T(8,128)(2,1)S(1)} %reshape.61, bf16[1,5120,2048]{2,1,0:T(8,128)(2,1)} %param.17), kind=kOutput, calls=%fused_computation.26 | convolution fusion | flops 2013265920 | bytes 22740992 | tf_op jit(solution)/shard_map/dot_general | solution.py:121
  45.6 11.1 %fusion.31 = bf16[96,2048]{1,0:T(8,128)(2,1)S(1)} fusion(bf16[96,5120]{1,0:T(8,128)(2,1)S(1)} %reshape.61, bf16[1,5120,2048]{2,1,0:T(8,128)(2,1)} %param.18, f32[96,2048]{1,0:T(8,128)S(1)} %fusion.23), kind=kOutput, calls=%fused_computation.31 | convolution fusion | flops 2014445568 | bytes 23134208 | tf_op jit(solution)/shard_map/dot_general | solution.py:122
  56.8 2.4 %all_gather.11 = bf16[96,4096]{1,0:T(8,128)(2,1)S(1)} all-gather(bf16[96,2048]{1,0:T(8,128)(2,1)S(1)} %fusion.31), channel_id=1, replica_groups=mesh['ctx'=16,'tp'=2] {'tp'}, dimensions={1}, use_global_device_ids=true | all-gather | bytes 1179648 | tf_op jit(solution)/shard_map/all_gather | solution.py:124
  59.2 3.4 %fusion.25 = bf16[96,2560]{1,0:T(8,128)(2,1)S(1)} fusion(bf16[96,4096]{1,0:T(8,128)(2,1)S(1)} %all_gather.11, bf16[1,4096,2560]{2,1,0:T(8,128)(2,1)S(1)} %bitcast.57), kind=kOutput, calls=%fused_computation.28 | convolution fusion | flops 2013511680 | bytes 22249472 | tf_op jit(solution)/shard_map/dot_general | solution.py:125
  62.6 1.0 reshape.62
  63.6 9.6 %all-to-all-start.1 = ((bf16[16,6,2560]{2,1,0:T(8,128)(2,1)}), bf16[16,6,2560]{2,1,0:T(8,128)(2,1)S(1)}, u32[]{:S(2)}, u32[]{:S(2)}) async-start(bf16[16,6,2560]{2,1,0:T(8,128)(2,1)} %reshape.62), calls=%async_computation.1 | async-start | bytes 1310720 | tf_op jit(solution)/shard_map/all_to_all | solution.py:129
  73.4 2.9 %collective-permute-start.3 = (bf16[512,256]{0,1:T(8,128)(2,1)S(1)}, bf16[512,256]{0,1:T(8,128)(2,1)S(1)}, u32[]{:S(2)}, u32[]{:S(2)}) collective-permute-start(bf16[512,256]{0,1:T(8,128)(2,1)S(1)} %pad_maximum_fusion), channel_id=1, source_target_pairs={{0,16},{2,18},{4,20},{6,22},{8,24},{10,26},{12,28},{14,30},{16,0},... | collective-permute-start | bytes 786440 | tf_op jit(solution)/shard_map/ppermute | solution.py:18
  78.8 48.7 %all_gather.9 = bf16[1024,256]{1,0:T(8,128)(2,1)S(1)} all-gather(bf16[64,256]{1,0:T(8,128)(2,1)S(1)} %copy-done.5), channel_id=1, replica_groups=mesh['ctx'=16,'tp'=2] {'ctx'}, dimensions={0}, use_global_device_ids=true | all-gather | bytes 557056 | tf_op jit(solution)/shard_map/all_gather | solution.py:46
  127.5 1.6 %concatenate.21 = bf16[2048,256]{0,1:T(8,128)(2,1)S(1)} concatenate(bf16[64,256]{0,1:T(8,128)(2,1)S(1)} %copy.23, bf16[64,256]{0,1:T(8,128)(2,1)S(1)} %collective-permute-done, bf16[128,256]{0,1:T(8,128)(2,1)S(1)} %collective-permute-done.1, bf16[256,256]{0,1:T(8,128)(2,1)S(1)} %collective-permute-done.2, bf16[512,256]{0,1:T(8,128)(2,1)S(1)} %collective-permute-done.3, ...), dimensions={0} | concatenate | bytes 2097152 | tf_op jit(solution)/shard_map/jit(_roll_dynamic)/concatenate | solution.py:22
  129.2 6.6 %conditional.1 = ((f32[2,5,64]{2,1,0:T(8,128)S(1)}, f32[64,2,5,128]{3,0,2,1:T(8,128)S(1)})) conditional(s32[]{:T(128)} %convert_element_type.35, (f32[2,5,64]{2,1,0:T(8,128)S(1)}, f32[64,2,5,128]{3,0,2,1:T(8,128)S(1)}) %tuple.39, (s32[64]{0:T(128)S(1)}, s32[1024]{0:T(1024)S(1)}, bf16[1024,256]{1,0:T(8,128)(2,1)S(1)}, ...), branch_computations={%region_2.3_spmd, %region_3.6_spmd.clone} | conditional | flops 344295296 | bytes 22940116 | solution.py:89
  130.5 1.5 %copy-done.2 = f32[2,1024,64,5]{1,2,3,0:T(8,128)} copy-done((f32[2,1024,64,5]{1,2,3,0:T(8,128)}, f32[2,1024,64,5]{1,2,3,0:T(8,128)S(1)}, u32[]{:S(2)}) %copy-start.2) | copy-done | bytes 2621464 | tf_op jit(solution)/shard_map/while/body/eval_jaxpr/cond
  132.0 0.8 fusion.2
  133.1 2.6 %fusion.9 = f32[64,2,5,128]{3,0,2,1:T(8,128)S(1)} fusion(bf16[1024,2,128,1]{0,2,3,1:T(8,128)(2,1)S(1)} %bitcast.59, f32[2,1024,64,5]{1,2,3,0:T(8,128)} %copy-done.2, f32[2,5,64]{2,1,0:T(8,128)S(1)} %broadcast_maximum_fusion, pred[64,1024]{1,0:T(8,128)(4,1)S(1)} %broadcast_compare_fusion, f32[64,2,5,128]{3,0,2,1:T(8,128)S(1)} %get-tuple-element.200, ...), kind=kOutput, calls=%fused_computation.9 | convolution fusion | flops 171212800 | bytes 3871744 | tf_op jit(solution)/shard_map/while/body/eval_jaxpr/cond/branch_1_fun/hgqk,khd->qhgd/dot_general | solution.py:77
  136.0 0.9 convert_element_type.37
  137.0 0.8 gather_fusion
  137.9 0.8 multiply_convert_fusion
  (58 shorter events, 5.8 us)
Async XLA Ops:
  0.6 2.4 %copy-start = (bf16[64,2560]{1,0:T(8,128)(2,1)S(1)}, bf16[64,2560]{1,0:T(8,128)(2,1)}, u32[]{:S(2)}) copy-start(bf16[64,2560]{1,0:T(8,128)(2,1)} %param.14) | copy-start | bytes 983044
  0.6 24.7 %copy-start.6 = (s32[64,1]{0,1:T(1,128)S(1)}, s32[64,1]{0,1:T(1,128)}, u32[]{:S(2)}) copy-start(s32[64,1]{0,1:T(1,128)} %param.15) | copy-start | bytes 772
  0.7 12.0 %copy-start.4 = (bf16[64,256]{1,0:T(8,128)(2,1)S(1)}, bf16[64,256]{1,0:T(8,128)(2,1)}, u32[]{:S(2)}) copy-start(bf16[64,256]{1,0:T(8,128)(2,1)} %param.13) | copy-start | bytes 98308
  4.3 29.2 %all-to-all-start = ((bf16[16,6,2560]{2,1,0:T(8,128)(2,1)}), bf16[16,6,2560]{2,1,0:T(8,128)(2,1)S(1)}, u32[]{:S(2)}, u32[]{:S(2)}) async-start(bf16[16,6,2560]{2,1,0:T(8,128)(2,1)} %reshape_reshape.3), calls=%async_computation | async-start | bytes 1310720 | tf_op jit(solution)/shard_map/all_to_all | solution.py:117
  12.8 12.3 %collective-permute-start = (bf16[64,256]{0,1:T(8,128)(2,1)S(1)}, bf16[64,256]{0,1:T(8,128)(2,1)S(1)}, u32[]{:S(2)}, u32[]{:S(2)}) collective-permute-start(bf16[64,256]{0,1:T(8,128)(2,1)S(1)} %copy.23), channel_id=1, source_target_pairs={{0,30},{2,0},{4,2},{6,4},{8,6},{10,8},{12,10},{14,12},{16,14},{18,... | collective-permute-start | bytes 98312 | tf_op jit(solution)/shard_map/ppermute | solution.py:18
  25.3 4.7 %collective-permute-start.1 = (bf16[128,256]{0,1:T(8,128)(2,1)S(1)}, bf16[128,256]{0,1:T(8,128)(2,1)S(1)}, u32[]{:S(2)}, u32[]{:S(2)}) collective-permute-start(bf16[128,256]{0,1:T(8,128)(2,1)S(1)} %pad_maximum_fusion.2), channel_id=1, source_target_pairs={{0,28},{2,30},{4,0},{6,2},{8,4},{10,6},{12,8},{14,10},{16,12},{18,... | collective-permute-start | bytes 196616 | tf_op jit(solution)/shard_map/ppermute | solution.py:18
  30.0 43.2 %collective-permute-start.2 = (bf16[256,256]{0,1:T(8,128)(2,1)S(1)}, bf16[256,256]{0,1:T(8,128)(2,1)S(1)}, u32[]{:S(2)}, u32[]{:S(2)}) collective-permute-start(bf16[256,256]{0,1:T(8,128)(2,1)S(1)} %pad_maximum_fusion.1), channel_id=1, source_target_pairs={{0,24},{2,26},{4,28},{6,30},{8,0},{10,2},{12,4},{14,6},{16,8},{18,... | collective-permute-start | bytes 393224 | tf_op jit(solution)/shard_map/ppermute | solution.py:18
  36.7 22.5 %slice-start = ((s8[20971520]{0:T(1024)(128)(4,1)}), s8[4194304]{0:T(1024)(128)(4,1)S(1)}, s32[]{:S(2)}) async-start(s8[20971520]{0:T(1024)(128)(4,1)} %bitcast.56), calls=%async_computation.2 | async-start | bytes 8388608
  36.7 22.5 %slice-start.1 = ((s8[20971520]{0:T(1024)(128)(4,1)}), s8[4194304]{0:T(1024)(128)(4,1)S(1)}, s32[]{:S(2)}) async-start(s8[20971520]{0:T(1024)(128)(4,1)} %bitcast.56), calls=%async_computation.3 | async-start | bytes 8388608
  36.7 22.5 %slice-start.2 = ((s8[20971520]{0:T(1024)(128)(4,1)}), s8[4194304]{0:T(1024)(128)(4,1)S(1)}, s32[]{:S(2)}) async-start(s8[20971520]{0:T(1024)(128)(4,1)} %bitcast.56), calls=%async_computation.4 | async-start | bytes 8388608
  45.6 13.5 %slice-start.3 = ((s8[20971520]{0:T(1024)(128)(4,1)}), s8[4194304]{0:T(1024)(128)(4,1)S(1)}, s32[]{:S(2)}) async-start(s8[20971520]{0:T(1024)(128)(4,1)} %bitcast.56), calls=%async_computation.5 | async-start | bytes 8388608
  45.6 13.5 %slice-start.4 = ((s8[20971520]{0:T(1024)(128)(4,1)}), s8[4194304]{0:T(1024)(128)(4,1)S(1)}, s32[]{:S(2)}) async-start(s8[20971520]{0:T(1024)(128)(4,1)} %bitcast.56), calls=%async_computation.6 | async-start | bytes 8388608
  62.6 16.2 %copy-start.5 = (bf16[64,256]{1,0:T(8,128)(2,1)S(1)}, bf16[64,256]{1,0:T(8,128)(2,1)}, u32[]{:S(2)}) copy-start(bf16[64,256]{1,0:T(8,128)(2,1)} %param.12) | copy-start | bytes 98308
  63.6 65.5 %copy-start.3 = (bf16[64,1280]{1,0:T(8,128)(2,1)S(1)}, bf16[64,1280]{1,0:T(8,128)(2,1)}, u32[]{:S(2)}) copy-start(bf16[64,1280]{1,0:T(8,128)(2,1)} %param.11) | copy-start | bytes 491524
  63.6 73.3 %all-to-all-start.1 = ((bf16[16,6,2560]{2,1,0:T(8,128)(2,1)}), bf16[16,6,2560]{2,1,0:T(8,128)(2,1)S(1)}, u32[]{:S(2)}, u32[]{:S(2)}) async-start(bf16[16,6,2560]{2,1,0:T(8,128)(2,1)} %reshape.62), calls=%async_computation.1 | async-start | bytes 1310720 | tf_op jit(solution)/shard_map/all_to_all | solution.py:129
  73.4 54.1 %collective-permute-start.3 = (bf16[512,256]{0,1:T(8,128)(2,1)S(1)}, bf16[512,256]{0,1:T(8,128)(2,1)S(1)}, u32[]{:S(2)}, u32[]{:S(2)}) collective-permute-start(bf16[512,256]{0,1:T(8,128)(2,1)S(1)} %pad_maximum_fusion), channel_id=1, source_target_pairs={{0,16},{2,18},{4,20},{6,22},{8,24},{10,26},{12,28},{14,30},{16,0},... | collective-permute-start | bytes 786440 | tf_op jit(solution)/shard_map/ppermute | solution.py:18
  130.5 1.5 %copy-start.2 = (f32[2,1024,64,5]{1,2,3,0:T(8,128)}, f32[2,1024,64,5]{1,2,3,0:T(8,128)S(1)}, u32[]{:S(2)}) copy-start(f32[2,1024,64,5]{1,2,3,0:T(8,128)S(1)} %get-tuple-element.223) | copy-start | bytes 7864324 | tf_op jit(solution)/shard_map/while/body/eval_jaxpr/cond
  136.9 1.8 %copy-start.1 = (bf16[64,2560]{1,0:T(8,128)(2,1)S(1)}, bf16[64,2560]{1,0:T(8,128)(2,1)}, u32[]{:S(2)}) copy-start(bf16[64,2560]{1,0:T(8,128)(2,1)} %param.14) | copy-start | bytes 983044
  137.0 0.8 copy-start.7
